TPU v7x, 32 devices: a whole 2x2x4 slice. The times are simulated.
32 devices in a mesh: task: 4 (over z), mp: 8 (over y, x, core).
Axes of the slice: x: 2, y: 2, z: 4, core: 2. Of those that a mesh axis runs over, the one named last changes fastest.
Arguments:
- deter: float32 [1024, 4096], P('task', 'mp'), may hold values from -3 to 3
- draws: int32 [4, 32, 1024], P(None, None, 'task'), may hold values from 0 to 31
- actions: int32 [4, 1024], P(None, 'task'), may hold values from 0 to 17
- horizons: int32 [64], replicated, may hold values from 5 to 30, as said below
- offsets: int32 [4, 4], replicated, may hold values from 0 to 3, as said below
- embed_stoch: bfloat16 [1024, 1024], replicated, may hold values from -1 to 1
- embed_act: bfloat16 [18, 1024], replicated, may hold values from -6 to 6
- gru_weight: bfloat16 [5120, 3, 4096], P(None, None, 'mp'), may hold values from -0.078125 to 0.078125
- prior_weight: bfloat16 [4096, 1024], replicated, may hold values from -0.09375 to 0.09375
- logit_weight: bfloat16 [1024, 1024], replicated, may hold values from -0.75 to 0.75
- head_weight: bfloat16 [1024, 2], replicated, may hold values from -0.375 to 0.375
Outputs:
- log_prob: float32 [4, 1024], P(None, 'task')
- reward: float32 [4, 1024], P(None, 'task')
- continuation: float32 [4, 1024], P(None, 'task')
- final_deter: float32 [1024, 4096], P('task', 'mp')
Inputs may be any that keep to these rules, and one draw needn't show every extreme that they name: `horizons`: rows of task k are home rows k * (16) up to (k + 1) * 16 - 1. `offsets`: the 4 numbers of one row are distinct.
All inputs are finite; a program needn't handle non-finite values.
Results may differ from a plain program's by a relative error of at most 0.0045.
Values may be sent and summed in bfloat16 or wider, within the bound.
A program may use at most 128 MiB of HBM per device.

v0:
```python
import jax
import jax.numpy as jnp
from jax import lax
from jax.sharding import PartitionSpec as P

HID = 1024
GROUPS = 32
CLASSES = 32
ACTS = 18
TASKS = 64
BLK_DEV = 4
STEPS = 4
WSTART = 16


def normed_rows(values):
    entries = values.shape[-1]
    average = jnp.sum(values, axis=-1, keepdims=True) / entries
    squares = jnp.sum(values * values, axis=-1, keepdims=True) / entries
    return (values - average) * lax.rsqrt(squares - average * average + 1e-05)


def product(rows_in, weight):
    return jnp.dot(rows_in, weight, preferred_element_type=jnp.float32)


def recurrence(deter, embedded, gate_weight, living, det_full):
    carried = deter
    rows_here, det_share = deter.shape
    lows = []
    for moment in range(STEPS):
        low = carried.astype(jnp.bfloat16)
        gathered = lax.all_gather(low, "mp", axis=1, tiled=True)
        lows.append(gathered)
        joined = jnp.concatenate([embedded[moment], gathered], axis=1)
        parts = [product(joined, gate_weight[part]) for part in range(3)]
        sums = sum((jnp.sum(part, axis=1) for part in parts))
        squares = sum((jnp.sum(part * part, axis=1) for part in parts))
        sums, squares = lax.psum(jnp.stack([sums, squares]), "mp")
        average = sums / (3 * det_full)
        inverse = lax.rsqrt(squares / (3 * det_full) - average * average + 1e-05)
        normed = [(part - average[:, None]) * inverse[:, None] for part in parts]
        reset_gate = jax.nn.sigmoid(normed[0])
        candidate = jnp.tanh(reset_gate * normed[1])
        update = jax.nn.sigmoid(normed[2] - 1.0)
        renewed = update * candidate + (1.0 - update) * carried
        carried = jnp.where(living[moment][:, None] > 0, renewed, carried)
    return (carried, lows)


def on_device(
    deter,
    draws,
    actions,
    horizons,
    offsets,
    embed_stoch,
    embed_act,
    gru_weight,
    prior_weight,
    logit_weight,
    head_weight,
):
    holders = lax.axis_size("task")
    device = lax.axis_index("task")
    shards = lax.axis_size("mp")
    shard_index = lax.axis_index("mp")
    rows_here, det_share = deter.shape
    block_rows = rows_here // BLK_DEV
    per_task = rows_here * holders // TASKS
    own_rows = rows_here // shards
    places = jnp.arange(holders, dtype=jnp.int32)
    classes = jnp.arange(CLASSES, dtype=jnp.int32)
    running = jnp.cumsum(offsets, axis=0) % holders
    packed = jnp.concatenate([draws, actions[:, None]], axis=1).astype(jnp.bfloat16)
    packed = lax.all_gather(packed, "task")
    packed = packed.reshape(holders, STEPS, GROUPS + 1, BLK_DEV, block_rows)
    at_slot = (device + running) % holders
    picked = places[:, None, None] == at_slot[None]
    packed = jnp.sum(
        jnp.where(picked[:, :, None, :, None], packed.astype(jnp.float32), 0.0), axis=0
    ).astype(jnp.int32)
    packed = packed.reshape(STEPS, GROUPS + 1, rows_here)
    draws_home = jnp.transpose(packed[:, :GROUPS], (0, 2, 1))
    hot = (draws_home[:, :, :, None] == classes).astype(jnp.bfloat16)
    hot = hot.reshape(STEPS * rows_here, GROUPS * CLASSES)
    action_hot = (
        packed[:, GROUPS].reshape(-1)[:, None] == jnp.arange(ACTS, dtype=jnp.int32)
    ).astype(jnp.bfloat16)
    embed_pre = product(hot, embed_stoch) + product(action_hot, embed_act)
    embedded = jax.nn.silu(normed_rows(embed_pre)).astype(jnp.bfloat16)
    embedded = embedded.reshape(STEPS, rows_here, HID)
    home_rows = device * rows_here + jnp.arange(rows_here, dtype=jnp.int32)
    task_ids = jnp.arange(TASKS, dtype=jnp.int32)
    horizon_rows = jnp.sum(
        jnp.where((home_rows // per_task)[:, None] == task_ids, horizons, 0), axis=1
    )
    alive = horizon_rows[None] > WSTART + jnp.arange(STEPS, dtype=jnp.int32)[:, None]
    living = alive.astype(jnp.float32)
    gate_weight = jnp.transpose(gru_weight, (1, 0, 2))
    carried, lows = recurrence(deter, embedded, gate_weight, living, det_share * shards)
    target = (device + running[-1]) % holders
    sending = places[:, None] == target[None, :]
    blocks = carried.reshape(BLK_DEV, block_rows, det_share)
    outgoing = jnp.where(sending[:, :, None, None], blocks[None], 0.0).astype(jnp.bfloat16)
    arrived = lax.all_to_all(
        outgoing.reshape(holders * BLK_DEV * block_rows, det_share),
        "task",
        split_axis=0,
        concat_axis=0,
        tiled=True,
    ).reshape(holders, BLK_DEV, block_rows, det_share)
    taking = places[:, None] == ((device - running[-1]) % holders)[None, :]
    final = jnp.sum(
        jnp.where(taking[:, :, None, None], arrived.astype(jnp.float32), 0.0), axis=0
    ).reshape(rows_here, det_share)

    def own(array, axis):
        return lax.dynamic_slice_in_dim(array, shard_index * own_rows, own_rows, axis)

    state_rows = jnp.concatenate([own(low, 0) for low in lows], axis=0)
    hidden = jax.nn.silu(normed_rows(product(state_rows, prior_weight))).astype(jnp.bfloat16)
    raw = product(hidden, logit_weight).reshape(STEPS * own_rows, GROUPS, CLASSES)
    exponent = jnp.exp(5.0 * jnp.tanh(raw / 5.0))
    own_hot = own(draws_home, 1).reshape(STEPS * own_rows, GROUPS)[:, :, None] == classes
    chosen = jnp.sum(jnp.where(own_hot, exponent, 0.0), axis=-1)
    chances = 0.99 * chosen / jnp.sum(exponent, axis=-1) + 0.01 / CLASSES
    log_prob = jnp.sum(jnp.log(chances), axis=-1)
    head_out = product(hidden, head_weight)
    results = jnp.stack([log_prob, head_out[:, 0], jax.nn.sigmoid(head_out[:, 1])])
    results = results.reshape(3, STEPS, own_rows) * own(living, 1)[None]
    spread = lax.all_gather(results, ("task", "mp"))
    spread = spread.reshape(holders, shards, 3, STEPS, own_rows)
    spread = jnp.transpose(spread, (0, 2, 3, 1, 4)).reshape(holders, 3, STEPS, BLK_DEV, block_rows)
    source = (device - running) % holders
    from_home = places[:, None, None] == source[None]
    outs = jnp.sum(jnp.where(from_home[:, None, :, :, None], spread, 0.0), axis=0)
    outs = outs.reshape(3, STEPS, rows_here)
    return (outs[0], outs[1], outs[2], final)


def solution(mesh):
    in_specs = (
        P("task", "mp"),
        P(None, None, "task"),
        P(None, "task"),
        P(),
        P(),
        P(),
        P(),
        P(None, None, "mp"),
        P(),
        P(),
        P(),
    )
    out_specs = (P(None, "task"), P(None, "task"), P(None, "task"), P("task", "mp"))
    return jax.shard_map(
        on_device, mesh=mesh, in_specs=in_specs, out_specs=out_specs, check_vma=False
    )
```

profile of v0, /device:TPU:0, one launch (start us, length us, event | category | flops | bytes accessed | tf_op | source)
XLA Modules:
  0.0 310.5 jit_solution(17363063580489032251)
XLA Ops:
  12.0 15.7 %all_gather.20 = bf16[4,4,33,256]{3,1,2,0:T(4,128)(2,1)S(1)} all-gather(bf16[1,4,33,256]{3,1,2,0:T(4,128)(2,1)S(1)} %pad_maximum_fusion.16), channel_id=1, replica_groups=mesh['task'=4,'mp'=8] {'task'}, dimensions={0}, use_global_device_ids=true | all-gather | bytes 337920 | tf_op jit(solution)/shard_map/all_gather | solution.py:76
  36.5 4.2 %all-gather.5.cloned.1.call-done = bf16[256,4096]{1,0:T(8,128)(2,1)} async-done(((bf16[256,512]{1,0:T(8,128)(2,1)}), bf16[256,4096]{1,0:T(8,128)(2,1)}) %all-gather.5.cloned.1.call-update) | async-done | bytes 2097168 | tf_op jit(solution)/shard_map/all_gather | solution.py:33
  40.7 4.9 %fusion.59 = (f32[256]{0:T(256)S(1)}, f32[256]{0:T(256)S(1)}, f32[256,512]{1,0:T(8,128)S(1)}) fusion(bf16[3,5120,512]{2,1,0:T(8,128)(2,1)} %bitcast.126, bf16[256,4096]{1,0:T(8,128)(2,1)} %all-gather.5.cloned.1.call-done, bf16[256,1024]{1,0:T(8,128)(2,1)S(1)} %copy.60), kind=kOutput, calls=%fused_computation.170 | convolution fusion | flops 1347812864 | bytes 8390656 | tf_op jit(solution)/shard_map/dot_general | solution.py:24
  45.6 4.8 %fusion.58 = (f32[256]{0:T(256)S(1)}, f32[256]{0:T(256)S(1)}, f32[256,512]{1,0:T(8,128)}) fusion(bf16[3,5120,512]{2,1,0:T(8,128)(2,1)} %bitcast.127, bf16[256,4096]{1,0:T(8,128)(2,1)S(1)} %copy-done.5, bf16[256,1024]{1,0:T(8,128)(2,1)S(1)} %copy.60), kind=kOutput, calls=%fused_computation.169 | convolution fusion | flops 1347812864 | bytes 8390656 | tf_op jit(solution)/shard_map/dot_general | solution.py:24
  50.4 4.9 %fusion.60 = (f32[256]{0:T(256)S(1)}, f32[256]{0:T(256)S(1)}, f32[256,512]{1,0:T(8,128)}) fusion(bf16[3,5120,512]{2,1,0:T(8,128)(2,1)} %bitcast.128, bf16[256,4096]{1,0:T(8,128)(2,1)S(1)} %copy-done.5, bf16[256,1024]{1,0:T(8,128)(2,1)S(1)} %copy.60), kind=kOutput, calls=%fused_computation.171 | convolution fusion | flops 1347812864 | bytes 8390656 | tf_op jit(solution)/shard_map/dot_general | solution.py:24
  55.4 13.1 %psum.28 = f32[2,256]{1,0:T(2,128)S(1)} all-reduce(f32[2,256]{1,0:T(2,128)S(1)} %pad_maximum_fusion.17), channel_id=1, replica_groups=mesh['task'=4,'mp'=8] {'mp'}, use_global_device_ids=true, to_apply=%region_11.12 | all-reduce | flops 512 | bytes 4096 | tf_op jit(solution)/shard_map/psum | solution.py:39
  71.3 27.8 %all-gather.7.cloned.1.call-done = bf16[256,4096]{1,0:T(8,128)(2,1)} async-done(((bf16[256,512]{1,0:T(8,128)(2,1)}), bf16[256,4096]{1,0:T(8,128)(2,1)}) %all-gather.7.cloned.1.call-update) | async-done | bytes 2097168 | tf_op jit(solution)/shard_map/all_gather | solution.py:33
  99.1 4.9 %fusion.56 = (f32[256]{0:T(256)S(1)}, f32[256]{0:T(256)S(1)}, f32[256,512]{1,0:T(8,128)S(1)}) fusion(bf16[3,5120,512]{2,1,0:T(8,128)(2,1)} %bitcast.129, bf16[256,4096]{1,0:T(8,128)(2,1)} %all-gather.7.cloned.1.call-done, bf16[256,1024]{1,0:T(8,128)(2,1)S(1)} %copy.61), kind=kOutput, calls=%fused_computation.167 | convolution fusion | flops 1347812864 | bytes 8390656 | tf_op jit(solution)/shard_map/dot_general | solution.py:24
  104.0 4.8 %fusion.55 = (f32[256]{0:T(256)S(1)}, f32[256]{0:T(256)S(1)}, f32[256,512]{1,0:T(8,128)}) fusion(bf16[3,5120,512]{2,1,0:T(8,128)(2,1)} %bitcast.130, bf16[256,4096]{1,0:T(8,128)(2,1)S(1)} %copy-done.6, bf16[256,1024]{1,0:T(8,128)(2,1)S(1)} %copy.61), kind=kOutput, calls=%fused_computation.166 | convolution fusion | flops 1347812864 | bytes 8390656 | tf_op jit(solution)/shard_map/dot_general | solution.py:24
  108.8 4.8 %fusion.57 = (f32[256]{0:T(256)S(1)}, f32[256]{0:T(256)S(1)}, f32[256,512]{1,0:T(8,128)}) fusion(bf16[3,5120,512]{2,1,0:T(8,128)(2,1)} %bitcast.131, bf16[256,4096]{1,0:T(8,128)(2,1)S(1)} %copy-done.6, bf16[256,1024]{1,0:T(8,128)(2,1)S(1)} %copy.61), kind=kOutput, calls=%fused_computation.168 | convolution fusion | flops 1347812864 | bytes 8390656 | tf_op jit(solution)/shard_map/dot_general | solution.py:24
  113.7 13.1 %psum.29 = f32[2,256]{1,0:T(2,128)S(1)} all-reduce(f32[2,256]{1,0:T(2,128)S(1)} %pad_maximum_fusion.18), channel_id=1, replica_groups=mesh['task'=4,'mp'=8] {'mp'}, use_global_device_ids=true, to_apply=%region_18.19 | all-reduce | flops 512 | bytes 4096 | tf_op jit(solution)/shard_map/psum | solution.py:39
  129.4 28.0 %all-gather.9.cloned.1.call-done = bf16[256,4096]{1,0:T(8,128)(2,1)} async-done(((bf16[256,512]{1,0:T(8,128)(2,1)}), bf16[256,4096]{1,0:T(8,128)(2,1)}) %all-gather.9.cloned.1.call-update) | async-done | bytes 2097168 | tf_op jit(solution)/shard_map/all_gather | solution.py:33
  157.4 4.9 %fusion.53 = (f32[256]{0:T(256)S(1)}, f32[256]{0:T(256)S(1)}, f32[256,512]{1,0:T(8,128)S(1)}) fusion(bf16[3,5120,512]{2,1,0:T(8,128)(2,1)} %bitcast.132, bf16[256,4096]{1,0:T(8,128)(2,1)} %all-gather.9.cloned.1.call-done, bf16[256,1024]{1,0:T(8,128)(2,1)S(1)} %copy.62), kind=kOutput, calls=%fused_computation.164 | convolution fusion | flops 1347812864 | bytes 8390656 | tf_op jit(solution)/shard_map/dot_general | solution.py:24
  162.4 4.1 %fusion.52 = (f32[256]{0:T(256)S(1)}, f32[256]{0:T(256)S(1)}, f32[256,512]{1,0:T(8,128)S(1)}) fusion(bf16[3,5120,512]{2,1,0:T(8,128)(2,1)} %bitcast.133, bf16[256,4096]{1,0:T(8,128)(2,1)S(1)} %copy-done.7, bf16[256,1024]{1,0:T(8,128)(2,1)S(1)} %copy.62), kind=kOutput, calls=%fused_computation.163 | convolution fusion | flops 1347812864 | bytes 8390656 | tf_op jit(solution)/shard_map/dot_general | solution.py:24
  166.5 4.8 %fusion.54 = (f32[256]{0:T(256)S(1)}, f32[256]{0:T(256)S(1)}, f32[256,512]{1,0:T(8,128)}) fusion(bf16[3,5120,512]{2,1,0:T(8,128)(2,1)} %bitcast.134, bf16[256,4096]{1,0:T(8,128)(2,1)S(1)} %copy-done.7, bf16[256,1024]{1,0:T(8,128)(2,1)S(1)} %copy.62), kind=kOutput, calls=%fused_computation.165 | convolution fusion | flops 1347812864 | bytes 8390656 | tf_op jit(solution)/shard_map/dot_general | solution.py:24
  171.3 13.1 %psum.30 = f32[2,256]{1,0:T(2,128)S(1)} all-reduce(f32[2,256]{1,0:T(2,128)S(1)} %pad_maximum_fusion.19), channel_id=1, replica_groups=mesh['task'=4,'mp'=8] {'mp'}, use_global_device_ids=true, to_apply=%region_25.26 | all-reduce | flops 512 | bytes 4096 | tf_op jit(solution)/shard_map/psum | solution.py:39
  192.0 22.9 %all-gather.11.cloned.1.call-done = bf16[256,4096]{1,0:T(8,128)(2,1)} async-done(((bf16[256,512]{1,0:T(8,128)(2,1)}), bf16[256,4096]{1,0:T(8,128)(2,1)}) %all-gather.11.cloned.1.call-update) | async-done | bytes 2097168 | tf_op jit(solution)/shard_map/all_gather | solution.py:33
  214.9 4.9 %fusion.49 = (f32[256]{0:T(256)S(1)}, f32[256]{0:T(256)S(1)}, f32[256,512]{1,0:T(8,128)S(1)}) fusion(bf16[3,5120,512]{2,1,0:T(8,128)(2,1)} %bitcast.135, bf16[256,4096]{1,0:T(8,128)(2,1)} %all-gather.11.cloned.1.call-done, bf16[256,1024]{1,0:T(8,128)(2,1)S(1)} %copy.67), kind=kOutput, calls=%fused_computation.160 | convolution fusion | flops 1347812864 | bytes 8390656 | tf_op jit(solution)/shard_map/dot_general | solution.py:24
  219.8 4.1 %fusion.48 = (f32[256]{0:T(256)S(1)}, f32[256]{0:T(256)S(1)}, f32[256,512]{1,0:T(8,128)S(1)}) fusion(bf16[3,5120,512]{2,1,0:T(8,128)(2,1)} %bitcast.136, bf16[256,4096]{1,0:T(8,128)(2,1)S(1)} %copy-done.8, bf16[256,1024]{1,0:T(8,128)(2,1)S(1)} %copy.67), kind=kOutput, calls=%fused_computation.159 | convolution fusion | flops 1347812864 | bytes 8390656 | tf_op jit(solution)/shard_map/dot_general | solution.py:24
  224.0 4.1 %fusion.50 = (f32[256]{0:T(256)S(1)}, f32[256]{0:T(256)S(1)}, f32[256,512]{1,0:T(8,128)S(1)}) fusion(bf16[3,5120,512]{2,1,0:T(8,128)(2,1)} %bitcast.137, bf16[256,4096]{1,0:T(8,128)(2,1)S(1)} %copy-done.8, bf16[256,1024]{1,0:T(8,128)(2,1)S(1)} %copy.67), kind=kOutput, calls=%fused_computation.161 | convolution fusion | flops 1347812864 | bytes 8390656 | tf_op jit(solution)/shard_map/dot_general | solution.py:24
  228.1 13.3 %psum.31 = f32[2,256]{1,0:T(2,128)S(1)} all-reduce(f32[2,256]{1,0:T(2,128)S(1)} %pad_maximum_fusion.20), channel_id=1, replica_groups=mesh['task'=4,'mp'=8] {'mp'}, use_global_device_ids=true, to_apply=%region_38.39 | all-reduce | flops 512 | bytes 4096 | tf_op jit(solution)/shard_map/psum | solution.py:39
  243.1 4.6 %all-to-all-start = ((bf16[4,256,512]{2,1,0:T(8,128)(2,1)}), bf16[4,256,512]{2,1,0:T(8,128)(2,1)S(1)}, u32[]{:S(2)}, u32[]{:S(2)}) async-start(bf16[4,256,512]{2,1,0:T(8,128)(2,1)} %select_convert_fusion), calls=%async_computation | async-start | bytes 2097152 | tf_op jit(solution)/shard_map/all_to_all | solution.py:106
  248.7 5.1 %fusion.51 = (f32[128]{0:T(128)S(1)}, f32[128]{0:T(128)S(1)}, f32[128,1024]{1,0:T(8,128)S(1)}) fusion(bf16[4096,1024]{1,0:T(8,128)(2,1)} %param.19, bf16[32,4096]{1,0:T(8,128)(2,1)S(1)} %constant_dynamic-slice_fusion.1, bf16[32,4096]{1,0:T(8,128)(2,1)} %constant_dynamic-slice_fusion.2, bf16[32,4096]{1,0:T(8,128)(2,1)} %constant_dynamic-slice_fusion.3, ...), kind=kOutput, calls=%fused_computation.162 | convolution fusion | flops 1078329088 | bytes 9962496 | tf_op jit(solution)/shard_map/dot_general | solution.py:24
  260.8 40.0 %all_gather.25 = f32[32,3,4,32]{3,2,1,0:T(4,128)S(1)} all-gather(f32[1,3,4,32]{3,2,1,0:T(4,128)S(1)} %maximum_multiply_fusion), channel_id=1, replica_groups=mesh['task'=4,'mp'=8] {'task','mp'}, dimensions={0}, use_global_device_ids=true | all-gather | bytes 50688 | tf_op jit(solution)/shard_map/all_gather | solution.py:132
  (128 shorter events, 39.4 us)
Async XLA Ops:
  7.2 22.4 %copy-start = (bf16[1024,1024]{1,0:T(8,128)(2,1)S(1)}, bf16[1024,1024]{1,0:T(8,128)(2,1)}, u32[]{:S(2)}) copy-start(bf16[1024,1024]{1,0:T(8,128)(2,1)} %param.16) | copy-start | bytes 6291460
  7.2 33.5 %all-gather.5.cloned.1.call-start = ((), (), s32[]{:S(2)}) async-start(), calls=%async_computation.1 | async-start | bytes 2359296 | tf_op jit(solution)/shard_map/all_gather | solution.py:33
  9.2 89.9 %all-gather.7.cloned.1.call-start = ((), (), s32[]{:S(2)}) async-start(), calls=%async_computation.2 | async-start | bytes 2359296 | tf_op jit(solution)/shard_map/all_gather | solution.py:33
  29.6 2.6 copy-start.4
  35.1 1.2 copy-start.10
  40.7 4.9 %copy-start.5 = (bf16[256,4096]{1,0:T(8,128)(2,1)S(1)}, bf16[256,4096]{1,0:T(8,128)(2,1)}, u32[]{:S(2)}) copy-start(bf16[256,4096]{1,0:T(8,128)(2,1)} %all-gather.5.cloned.1.call-done) | copy-start | bytes 6291460
  50.4 18.0 %copy-start.2 = (f32[256,512]{1,0:T(8,128)S(1)}, f32[256,512]{1,0:T(8,128)}, u32[]{:S(2)}) copy-start(f32[256,512]{1,0:T(8,128)} %param.11) | copy-start | bytes 1572868
  50.4 20.7 %copy-start.3 = (bf16[256,1024]{0,1:T(8,128)(2,1)S(1)}, bf16[256,1024]{0,1:T(8,128)(2,1)}, u32[]{:S(2)}) copy-start(bf16[256,1024]{0,1:T(8,128)(2,1)} %get-tuple-element.50) | copy-start | bytes 1572868
  70.9 86.6 %all-gather.9.cloned.1.call-start = ((), (), s32[]{:S(2)}) async-start(), calls=%async_computation.3 | async-start | bytes 2359296 | tf_op jit(solution)/shard_map/all_gather | solution.py:33
  99.1 4.9 %copy-start.6 = (bf16[256,4096]{1,0:T(8,128)(2,1)S(1)}, bf16[256,4096]{1,0:T(8,128)(2,1)}, u32[]{:S(2)}) copy-start(bf16[256,4096]{1,0:T(8,128)(2,1)} %all-gather.7.cloned.1.call-done) | copy-start | bytes 6291460
  129.2 85.7 %all-gather.11.cloned.1.call-start = ((), (), s32[]{:S(2)}) async-start(), calls=%async_computation.4 | async-start | bytes 2359296 | tf_op jit(solution)/shard_map/all_gather | solution.py:33
  157.4 4.9 %copy-start.7 = (bf16[256,4096]{1,0:T(8,128)(2,1)S(1)}, bf16[256,4096]{1,0:T(8,128)(2,1)}, u32[]{:S(2)}) copy-start(bf16[256,4096]{1,0:T(8,128)(2,1)} %all-gather.9.cloned.1.call-done) | copy-start | bytes 6291460
  214.9 4.9 %copy-start.8 = (bf16[256,4096]{1,0:T(8,128)(2,1)S(1)}, bf16[256,4096]{1,0:T(8,128)(2,1)}, u32[]{:S(2)}) copy-start(bf16[256,4096]{1,0:T(8,128)(2,1)} %all-gather.11.cloned.1.call-done) | copy-start | bytes 6291460
  243.1 59.8 %all-to-all-start = ((bf16[4,256,512]{2,1,0:T(8,128)(2,1)}), bf16[4,256,512]{2,1,0:T(8,128)(2,1)S(1)}, u32[]{:S(2)}, u32[]{:S(2)}) async-start(bf16[4,256,512]{2,1,0:T(8,128)(2,1)} %select_convert_fusion), calls=%async_computation | async-start | bytes 2097152 | tf_op jit(solution)/shard_map/all_to_all | solution.py:106
  248.7 5.4 %copy-start.9 = (bf16[1024,2]{0,1:T(2,128)(2,1)S(1)}, bf16[1024,2]{0,1:T(2,128)(2,1)}, u32[]{:S(2)}) copy-start(bf16[1024,2]{0,1:T(2,128)(2,1)} %param.21) | copy-start | bytes 12292
  248.7 55.3 %copy-start.1 = (bf16[1024,1024]{1,0:T(8,128)(2,1)S(1)}, bf16[1024,1024]{1,0:T(8,128)(2,1)}, u32[]{:S(2)}) copy-start(bf16[1024,1024]{1,0:T(8,128)(2,1)} %param.16) | copy-start | bytes 6291460
Sparse Core Ops, SparseCore 0:
  9.9 30.8 all-gather.4
  71.0 28.0 all-gather.6
  129.3 28.0 all-gather.8
  186.8 28.0 all-gather.10
where the time goes:
time: 312 us; the launch traced here: 311 us
  blocking collectives  108 us (35%)
  waiting for transfers between devices  83 us (27%)
  matrix products  68.2 us (22%)
  other arithmetic  17.7 us (6%)
  local copies, waits for them, and re-layouts  14.2 us (5%)
  between operations  14.2 us (5%)
  starting transfers between devices  4.94 us (2%)
    all_gather x4, waiting for transfers between devices, recurrence(): gathered = lax.all_gather(low, 'mp', axis=1, tiled=True)  83 us
    dot_general x17, matrix products, product(): return jnp.dot(rows_in, weight, preferred_element_type=jnp.float32)  68.2 us
    psum x4, blocking collectives, recurrence(): sums, squares = lax.psum(jnp.stack([sums, squares]), 'mp')  52.6 us
    all_gather x1, blocking collectives, on_device(): spread = lax.all_gather(results, ('task', 'mp'))  40 us
    all_gather x1, blocking collectives, on_device(): packed = lax.all_gather(packed, 'task')  15.7 us
    convert_element_type x4, other arithmetic, recurrence(): low = carried.astype(jnp.bfloat16)  8.9 us
  transfers between devices with their start and end apart: 5, of which 4 were waited for; matrix products, arithmetic and copies ran while one was open for 10% of the time, Pallas kernels for 0%

commit v1 on v0

--- a/solution.py
+++ b/solution.py
@@ -30,7 +30,14 @@
     lows = []
     for moment in range(STEPS):
         low = carried.astype(jnp.bfloat16)
-        gathered = lax.all_gather(low, "mp", axis=1, tiled=True)
+        n_dev = lax.axis_size("mp")
+        right = [(i, (i + 1) % n_dev) for i in range(n_dev)]
+        terms = [low]
+        for stride in range(1, n_dev):
+            terms = [lax.ppermute(terms[0], "mp", right), *terms]
+        result = jnp.concatenate(terms, axis=1)
+        shift = (lax.axis_index("mp") + 1) * terms[-1].shape[1]
+        gathered = jnp.roll(result, shift, axis=1)
         lows.append(gathered)
         joined = jnp.concatenate([embedded[moment], gathered], axis=1)
         parts = [product(joined, gate_weight[part]) for part in range(3)]

time: 312 us -> 415 us (1.33); the launches traced: 311 us -> 407 us
  waiting for transfers between devices: 83 us -> 164 us
  local copies, waits for them, and re-layouts: 14.2 us -> 32.9 us
  between operations: 14.2 us -> 1.83 us
  other arithmetic: 17.7 us -> 28.4 us
  blocking collectives: 108 us -> 103 us
    ppermute x0 -> x28, waiting for transfers between devices: none -> 164 us  [recurrence(): terms = [lax.ppermute(terms[0], 'mp', right), *terms]]
    all_gather x4 -> x0, waiting for transfers between devices: 83 us -> none  [recurrence(): gathered = lax.all_gather(low, 'mp', axis=1, tiled=True)]
    unnamed x24 -> x112, local copies, waits for them, and re-layouts: 1.12 us -> 19.7 us
    concatenate x0 -> x7, other arithmetic: none -> 8.41 us  [the longest x6 8.37 us: recurrence(): gathered = jnp.roll(result, shift, axis=1)]
    psum x4, blocking collectives: 52.6 us -> 47.2 us  [recurrence(): sums, squares = lax.psum(jnp.stack([sums, squares]), 'mp')]
    dynamic_slice x7 -> x3, local copies, waits for them, and re-layouts: 5.51 us -> 0.21 us  [own(): lax.dynamic_slice_in_dim(array, shard_index * own_rows, own_rows, axis)]
    slice x5, local copies, waits for them, and re-layouts: 1.75 us -> 5.97 us  [recurrence(): joined = jnp.concatenate([embedded[moment], gathered], axis=1)]
  transfers between devices with their start and end apart: 5 -> 29, of which waited for: 4 -> 27; matrix products, arithmetic and copies ran while one was open for 10% -> 9% of each run, Pallas kernels for 0% -> 0%
where the time goes in v1:
time: 415 us; the launch traced here: 407 us
  waiting for transfers between devices  164 us (40%)
  blocking collectives  103 us (25%)
  matrix products  69.9 us (17%)
  local copies, waits for them, and re-layouts  32.9 us (8%)
  other arithmetic  28.4 us (7%)
  starting transfers between devices  6.15 us (1%)
    ppermute x28, waiting for transfers between devices, recurrence(): terms = [lax.ppermute(terms[0], 'mp', right), *terms]  164 us
    dot_general x17, matrix products, product(): return jnp.dot(rows_in, weight, preferred_element_type=jnp.float32)  69.9 us
    psum x4, blocking collectives, recurrence(): sums, squares = lax.psum(jnp.stack([sums, squares]), 'mp')  47.2 us
    all_gather x1, blocking collectives, on_device(): spread = lax.all_gather(results, ('task', 'mp'))  40.5 us
    unnamed x112, local copies, waits for them, and re-layouts  19.7 us
    all_gather x1, blocking collectives, on_device(): packed = lax.all_gather(packed, 'task')  15.8 us
    concatenate x6, other arithmetic, recurrence(): gathered = jnp.roll(result, shift, axis=1)  8.37 us
  transfers between devices with their start and end apart: 29, of which 27 were waited for; matrix products, arithmetic and copies ran while one was open for 9% of the time, Pallas kernels for 0%

profile of v1, /device:TPU:0, one launch (start us, length us, event | category | flops | bytes accessed | tf_op | source)
XLA Modules:
  0.0 406.9 jit_solution(15461450892630545155)
XLA Ops:
  5.1 15.8 %all_gather.8 = bf16[4,4,33,256]{3,1,2,0:T(4,128)(2,1)S(1)} all-gather(bf16[1,4,33,256]{3,1,2,0:T(4,128)(2,1)S(1)} %pad_maximum_fusion.16), channel_id=1, replica_groups=mesh['task'=4,'mp'=8] {'task'}, dimensions={0}, use_global_device_ids=true | all-gather | bytes 337920 | tf_op jit(solution)/shard_map/all_gather | solution.py:83
  84.5 11.8 %psum.28 = f32[2,256]{1,0:T(2,128)S(1)} all-reduce(f32[2,256]{1,0:T(2,128)S(1)} %pad_maximum_fusion.17), channel_id=1, replica_groups=mesh['task'=4,'mp'=8] {'mp'}, use_global_device_ids=true, to_apply=%region_11.13 | all-reduce | flops 512 | bytes 4096 | tf_op jit(solution)/shard_map/psum | solution.py:46
  98.9 6.7 %collective-permute-done.7 = bf16[256,512]{1,0:T(8,128)(2,1)S(1)} collective-permute-done((bf16[256,512]{1,0:T(8,128)(2,1)S(1)}, bf16[256,512]{1,0:T(8,128)(2,1)S(1)}, u32[]{:S(2)}, u32[]{:S(2)}) %collective-permute-start.7) | collective-permute-done | bytes 262176 | tf_op jit(solution)/shard_map/ppermute | solution.py:37
  105.6 6.7 %collective-permute-done.8 = bf16[256,512]{1,0:T(8,128)(2,1)S(1)} collective-permute-done((bf16[256,512]{1,0:T(8,128)(2,1)S(1)}, bf16[256,512]{1,0:T(8,128)(2,1)S(1)}, u32[]{:S(2)}, u32[]{:S(2)}) %collective-permute-start.8) | collective-permute-done | bytes 262176 | tf_op jit(solution)/shard_map/ppermute | solution.py:37
  112.3 6.7 %collective-permute-done.9 = bf16[256,512]{1,0:T(8,128)(2,1)S(1)} collective-permute-done((bf16[256,512]{1,0:T(8,128)(2,1)S(1)}, bf16[256,512]{1,0:T(8,128)(2,1)S(1)}, u32[]{:S(2)}, u32[]{:S(2)}) %collective-permute-start.9) | collective-permute-done | bytes 262176 | tf_op jit(solution)/shard_map/ppermute | solution.py:37
  119.0 6.7 %collective-permute-done.10 = bf16[256,512]{1,0:T(8,128)(2,1)S(1)} collective-permute-done((bf16[256,512]{1,0:T(8,128)(2,1)S(1)}, bf16[256,512]{1,0:T(8,128)(2,1)S(1)}, u32[]{:S(2)}, u32[]{:S(2)}) %collective-permute-start.10) | collective-permute-done | bytes 262176 | tf_op jit(solution)/shard_map/ppermute | solution.py:37
  125.7 6.7 %collective-permute-done.11 = bf16[256,512]{1,0:T(8,128)(2,1)S(1)} collective-permute-done((bf16[256,512]{1,0:T(8,128)(2,1)S(1)}, bf16[256,512]{1,0:T(8,128)(2,1)S(1)}, u32[]{:S(2)}, u32[]{:S(2)}) %collective-permute-start.11) | collective-permute-done | bytes 262176 | tf_op jit(solution)/shard_map/ppermute | solution.py:37
  132.4 6.8 %collective-permute-done.12 = bf16[256,512]{1,0:T(8,128)(2,1)} collective-permute-done((bf16[256,512]{1,0:T(8,128)(2,1)S(1)}, bf16[256,512]{1,0:T(8,128)(2,1)}, u32[]{:S(2)}, u32[]{:S(2)}) %collective-permute-start.12) | collective-permute-done | bytes 262176 | tf_op jit(solution)/shard_map/ppermute | solution.py:37
  139.5 6.7 %collective-permute-done.13 = bf16[256,512]{1,0:T(8,128)(2,1)} collective-permute-done((bf16[256,512]{1,0:T(8,128)(2,1)}, bf16[256,512]{1,0:T(8,128)(2,1)}, u32[]{:S(2)}, u32[]{:S(2)}) %collective-permute-start.13) | collective-permute-done | bytes 262176 | tf_op jit(solution)/shard_map/ppermute | solution.py:37
  167.1 11.8 %psum.29 = f32[2,256]{1,0:T(2,128)S(1)} all-reduce(f32[2,256]{1,0:T(2,128)S(1)} %pad_maximum_fusion.18), channel_id=1, replica_groups=mesh['task'=4,'mp'=8] {'mp'}, use_global_device_ids=true, to_apply=%region_18.20 | all-reduce | flops 512 | bytes 4096 | tf_op jit(solution)/shard_map/psum | solution.py:46
  180.9 6.7 %collective-permute-done.14 = bf16[256,512]{1,0:T(8,128)(2,1)S(1)} collective-permute-done((bf16[256,512]{1,0:T(8,128)(2,1)S(1)}, bf16[256,512]{1,0:T(8,128)(2,1)S(1)}, u32[]{:S(2)}, u32[]{:S(2)}) %collective-permute-start.14) | collective-permute-done | bytes 262176 | tf_op jit(solution)/shard_map/ppermute | solution.py:37
  187.5 6.7 %collective-permute-done.15 = bf16[256,512]{1,0:T(8,128)(2,1)S(1)} collective-permute-done((bf16[256,512]{1,0:T(8,128)(2,1)S(1)}, bf16[256,512]{1,0:T(8,128)(2,1)S(1)}, u32[]{:S(2)}, u32[]{:S(2)}) %collective-permute-start.15) | collective-permute-done | bytes 262176 | tf_op jit(solution)/shard_map/ppermute | solution.py:37
  194.2 6.7 %collective-permute-done.16 = bf16[256,512]{1,0:T(8,128)(2,1)S(1)} collective-permute-done((bf16[256,512]{1,0:T(8,128)(2,1)S(1)}, bf16[256,512]{1,0:T(8,128)(2,1)S(1)}, u32[]{:S(2)}, u32[]{:S(2)}) %collective-permute-start.16) | collective-permute-done | bytes 262176 | tf_op jit(solution)/shard_map/ppermute | solution.py:37
  200.9 6.7 %collective-permute-done.17 = bf16[256,512]{1,0:T(8,128)(2,1)S(1)} collective-permute-done((bf16[256,512]{1,0:T(8,128)(2,1)S(1)}, bf16[256,512]{1,0:T(8,128)(2,1)S(1)}, u32[]{:S(2)}, u32[]{:S(2)}) %collective-permute-start.17) | collective-permute-done | bytes 262176 | tf_op jit(solution)/shard_map/ppermute | solution.py:37
  207.6 6.7 %collective-permute-done.18 = bf16[256,512]{1,0:T(8,128)(2,1)S(1)} collective-permute-done((bf16[256,512]{1,0:T(8,128)(2,1)S(1)}, bf16[256,512]{1,0:T(8,128)(2,1)S(1)}, u32[]{:S(2)}, u32[]{:S(2)}) %collective-permute-start.18) | collective-permute-done | bytes 262176 | tf_op jit(solution)/shard_map/ppermute | solution.py:37
  214.3 6.8 %collective-permute-done.19 = bf16[256,512]{1,0:T(8,128)(2,1)} collective-permute-done((bf16[256,512]{1,0:T(8,128)(2,1)S(1)}, bf16[256,512]{1,0:T(8,128)(2,1)}, u32[]{:S(2)}, u32[]{:S(2)}) %collective-permute-start.19) | collective-permute-done | bytes 262176 | tf_op jit(solution)/shard_map/ppermute | solution.py:37
  248.9 11.8 %psum.30 = f32[2,256]{1,0:T(2,128)S(1)} all-reduce(f32[2,256]{1,0:T(2,128)S(1)} %pad_maximum_fusion.19), channel_id=1, replica_groups=mesh['task'=4,'mp'=8] {'mp'}, use_global_device_ids=true, to_apply=%region_25.27 | all-reduce | flops 512 | bytes 4096 | tf_op jit(solution)/shard_map/psum | solution.py:46
  262.7 6.7 %collective-permute-done.21 = bf16[256,512]{1,0:T(8,128)(2,1)S(1)} collective-permute-done((bf16[256,512]{1,0:T(8,128)(2,1)S(1)}, bf16[256,512]{1,0:T(8,128)(2,1)S(1)}, u32[]{:S(2)}, u32[]{:S(2)}) %collective-permute-start.21) | collective-permute-done | bytes 262176 | tf_op jit(solution)/shard_map/ppermute | solution.py:37
  269.3 6.7 %collective-permute-done.22 = bf16[256,512]{1,0:T(8,128)(2,1)S(1)} collective-permute-done((bf16[256,512]{1,0:T(8,128)(2,1)S(1)}, bf16[256,512]{1,0:T(8,128)(2,1)S(1)}, u32[]{:S(2)}, u32[]{:S(2)}) %collective-permute-start.22) | collective-permute-done | bytes 262176 | tf_op jit(solution)/shard_map/ppermute | solution.py:37
  276.0 6.7 %collective-permute-done.23 = bf16[256,512]{1,0:T(8,128)(2,1)S(1)} collective-permute-done((bf16[256,512]{1,0:T(8,128)(2,1)S(1)}, bf16[256,512]{1,0:T(8,128)(2,1)S(1)}, u32[]{:S(2)}, u32[]{:S(2)}) %collective-permute-start.23) | collective-permute-done | bytes 262176 | tf_op jit(solution)/shard_map/ppermute | solution.py:37
  283.5 6.8 %collective-permute-done.24 = bf16[256,512]{1,0:T(8,128)(2,1)} collective-permute-done((bf16[256,512]{1,0:T(8,128)(2,1)S(1)}, bf16[256,512]{1,0:T(8,128)(2,1)}, u32[]{:S(2)}, u32[]{:S(2)}) %collective-permute-start.24) | collective-permute-done | bytes 262176 | tf_op jit(solution)/shard_map/ppermute | solution.py:37
  290.9 6.4 %collective-permute-done.25 = bf16[256,512]{1,0:T(8,128)(2,1)} collective-permute-done((bf16[256,512]{1,0:T(8,128)(2,1)}, bf16[256,512]{1,0:T(8,128)(2,1)}, u32[]{:S(2)}, u32[]{:S(2)}) %collective-permute-start.25) | collective-permute-done | bytes 262176 | tf_op jit(solution)/shard_map/ppermute | solution.py:37
  331.5 11.8 %psum.31 = f32[2,256]{1,0:T(2,128)S(1)} all-reduce(f32[2,256]{1,0:T(2,128)S(1)} %pad_maximum_fusion.20), channel_id=1, replica_groups=mesh['task'=4,'mp'=8] {'mp'}, use_global_device_ids=true, to_apply=%region_38.40 | all-reduce | flops 512 | bytes 4096 | tf_op jit(solution)/shard_map/psum | solution.py:46
  362.9 40.5 %all_gather.9 = f32[32,3,4,32]{3,2,1,0:T(4,128)S(1)} all-gather(f32[1,3,4,32]{3,2,1,0:T(4,128)S(1)} %maximum_multiply_fusion), channel_id=1, replica_groups=mesh['task'=4,'mp'=8] {'task','mp'}, dimensions={0}, use_global_device_ids=true | all-gather | bytes 50688 | tf_op jit(solution)/shard_map/all_gather | solution.py:139
  (266 shorter events, 181.1 us)
Async XLA Ops:
  1.9 20.9 %collective-permute-start = (bf16[256,512]{1,0:T(8,128)(2,1)S(1)}, bf16[256,512]{1,0:T(8,128)(2,1)S(1)}, u32[]{:S(2)}, u32[]{:S(2)}) collective-permute-start(bf16[256,512]{1,0:T(8,128)(2,1)S(1)} %convert_element_type.50), channel_id=1, source_target_pairs={{0,1},{1,2},{2,3},{3,4},{4,5},{5,6},{6,7},{7,0},{8,9},{9,10},{10,1... | collective-permute-start | bytes 786440 | tf_op jit(solution)/shard_map/ppermute | solution.py:37
  22.8 6.7 %collective-permute-start.1 = (bf16[256,512]{1,0:T(8,128)(2,1)S(1)}, bf16[256,512]{1,0:T(8,128)(2,1)S(1)}, u32[]{:S(2)}, u32[]{:S(2)}) collective-permute-start(bf16[256,512]{1,0:T(8,128)(2,1)S(1)} %collective-permute-done), channel_id=1, source_target_pairs={{0,1},{1,2},{2,3},{3,4},{4,5},{5,6},{6,7},{7,0},{8,9},{9,10},{10,1... | collective-permute-start | bytes 786440 | tf_op jit(solution)/shard_map/ppermute | solution.py:37
  29.6 6.7 %collective-permute-start.2 = (bf16[256,512]{1,0:T(8,128)(2,1)S(1)}, bf16[256,512]{1,0:T(8,128)(2,1)S(1)}, u32[]{:S(2)}, u32[]{:S(2)}) collective-permute-start(bf16[256,512]{1,0:T(8,128)(2,1)S(1)} %collective-permute-done.1), channel_id=1, source_target_pairs={{0,1},{1,2},{2,3},{3,4},{4,5},{5,6},{6,7},{7,0},{8,9},{9,10},{10,1... | collective-permute-start | bytes 786440 | tf_op jit(solution)/shard_map/ppermute | solution.py:37
  36.3 6.7 %collective-permute-start.3 = (bf16[256,512]{1,0:T(8,128)(2,1)S(1)}, bf16[256,512]{1,0:T(8,128)(2,1)S(1)}, u32[]{:S(2)}, u32[]{:S(2)}) collective-permute-start(bf16[256,512]{1,0:T(8,128)(2,1)S(1)} %collective-permute-done.2), channel_id=1, source_target_pairs={{0,1},{1,2},{2,3},{3,4},{4,5},{5,6},{6,7},{7,0},{8,9},{9,10},{10,1... | collective-permute-start | bytes 786440 | tf_op jit(solution)/shard_map/ppermute | solution.py:37
  43.0 6.8 %collective-permute-start.4 = (bf16[256,512]{1,0:T(8,128)(2,1)S(1)}, bf16[256,512]{1,0:T(8,128)(2,1)}, u32[]{:S(2)}, u32[]{:S(2)}) collective-permute-start(bf16[256,512]{1,0:T(8,128)(2,1)S(1)} %collective-permute-done.3), channel_id=1, source_target_pairs={{0,1},{1,2},{2,3},{3,4},{4,5},{5,6},{6,7},{7,0},{8,9},{9,10},{10,1... | collective-permute-start | bytes 786440 | tf_op jit(solution)/shard_map/ppermute | solution.py:37
  49.8 6.9 %collective-permute-start.5 = (bf16[256,512]{1,0:T(8,128)(2,1)}, bf16[256,512]{1,0:T(8,128)(2,1)S(1)}, u32[]{:S(2)}, u32[]{:S(2)}) collective-permute-start(bf16[256,512]{1,0:T(8,128)(2,1)} %collective-permute-done.4), channel_id=1, source_target_pairs={{0,1},{1,2},{2,3},{3,4},{4,5},{5,6},{6,7},{7,0},{8,9},{9,10},{10,1... | collective-permute-start | bytes 786440 | tf_op jit(solution)/shard_map/ppermute | solution.py:37
  56.7 7.1 %collective-permute-start.6 = (bf16[256,512]{1,0:T(8,128)(2,1)S(1)}, bf16[256,512]{1,0:T(8,128)(2,1)S(1)}, u32[]{:S(2)}, u32[]{:S(2)}) collective-permute-start(bf16[256,512]{1,0:T(8,128)(2,1)S(1)} %collective-permute-done.5), channel_id=1, source_target_pairs={{0,1},{1,2},{2,3},{3,4},{4,5},{5,6},{6,7},{7,0},{8,9},{9,10},{10,1... | collective-permute-start | bytes 786440 | tf_op jit(solution)/shard_map/ppermute | solution.py:37
  105.6 6.7 %collective-permute-start.8 = (bf16[256,512]{1,0:T(8,128)(2,1)S(1)}, bf16[256,512]{1,0:T(8,128)(2,1)S(1)}, u32[]{:S(2)}, u32[]{:S(2)}) collective-permute-start(bf16[256,512]{1,0:T(8,128)(2,1)S(1)} %collective-permute-done.7), channel_id=1, source_target_pairs={{0,1},{1,2},{2,3},{3,4},{4,5},{5,6},{6,7},{7,0},{8,9},{9,10},{10,1... | collective-permute-start | bytes 786440 | tf_op jit(solution)/shard_map/ppermute | solution.py:37
  112.3 6.7 %collective-permute-start.9 = (bf16[256,512]{1,0:T(8,128)(2,1)S(1)}, bf16[256,512]{1,0:T(8,128)(2,1)S(1)}, u32[]{:S(2)}, u32[]{:S(2)}) collective-permute-start(bf16[256,512]{1,0:T(8,128)(2,1)S(1)} %collective-permute-done.8), channel_id=1, source_target_pairs={{0,1},{1,2},{2,3},{3,4},{4,5},{5,6},{6,7},{7,0},{8,9},{9,10},{10,1... | collective-permute-start | bytes 786440 | tf_op jit(solution)/shard_map/ppermute | solution.py:37
  119.0 6.7 %collective-permute-start.10 = (bf16[256,512]{1,0:T(8,128)(2,1)S(1)}, bf16[256,512]{1,0:T(8,128)(2,1)S(1)}, u32[]{:S(2)}, u32[]{:S(2)}) collective-permute-start(bf16[256,512]{1,0:T(8,128)(2,1)S(1)} %collective-permute-done.9), channel_id=1, source_target_pairs={{0,1},{1,2},{2,3},{3,4},{4,5},{5,6},{6,7},{7,0},{8,9},{9,10},{10,1... | collective-permute-start | bytes 786440 | tf_op jit(solution)/shard_map/ppermute | solution.py:37
  125.7 6.7 %collective-permute-start.11 = (bf16[256,512]{1,0:T(8,128)(2,1)S(1)}, bf16[256,512]{1,0:T(8,128)(2,1)S(1)}, u32[]{:S(2)}, u32[]{:S(2)}) collective-permute-start(bf16[256,512]{1,0:T(8,128)(2,1)S(1)} %collective-permute-done.10), channel_id=1, source_target_pairs={{0,1},{1,2},{2,3},{3,4},{4,5},{5,6},{6,7},{7,0},{8,9},{9,10},{10,1... | collective-permute-start | bytes 786440 | tf_op jit(solution)/shard_map/ppermute | solution.py:37
  132.4 6.8 %collective-permute-start.12 = (bf16[256,512]{1,0:T(8,128)(2,1)S(1)}, bf16[256,512]{1,0:T(8,128)(2,1)}, u32[]{:S(2)}, u32[]{:S(2)}) collective-permute-start(bf16[256,512]{1,0:T(8,128)(2,1)S(1)} %collective-permute-done.11), channel_id=1, source_target_pairs={{0,1},{1,2},{2,3},{3,4},{4,5},{5,6},{6,7},{7,0},{8,9},{9,10},{10,1... | collective-permute-start | bytes 786440 | tf_op jit(solution)/shard_map/ppermute | solution.py:37
  139.2 7.0 %collective-permute-start.13 = (bf16[256,512]{1,0:T(8,128)(2,1)}, bf16[256,512]{1,0:T(8,128)(2,1)}, u32[]{:S(2)}, u32[]{:S(2)}) collective-permute-start(bf16[256,512]{1,0:T(8,128)(2,1)} %collective-permute-done.12), channel_id=1, source_target_pairs={{0,1},{1,2},{2,3},{3,4},{4,5},{5,6},{6,7},{7,0},{8,9},{9,10},{10,1... | collective-permute-start | bytes 786440 | tf_op jit(solution)/shard_map/ppermute | solution.py:37
  180.8 6.7 %collective-permute-start.14 = (bf16[256,512]{1,0:T(8,128)(2,1)S(1)}, bf16[256,512]{1,0:T(8,128)(2,1)S(1)}, u32[]{:S(2)}, u32[]{:S(2)}) collective-permute-start(bf16[256,512]{1,0:T(8,128)(2,1)S(1)} %get-tuple-element.45), channel_id=1, source_target_pairs={{0,1},{1,2},{2,3},{3,4},{4,5},{5,6},{6,7},{7,0},{8,9},{9,10},{10,1... | collective-permute-start | bytes 786440 | tf_op jit(solution)/shard_map/ppermute | solution.py:37
  194.2 6.7 %collective-permute-start.16 = (bf16[256,512]{1,0:T(8,128)(2,1)S(1)}, bf16[256,512]{1,0:T(8,128)(2,1)S(1)}, u32[]{:S(2)}, u32[]{:S(2)}) collective-permute-start(bf16[256,512]{1,0:T(8,128)(2,1)S(1)} %collective-permute-done.15), channel_id=1, source_target_pairs={{0,1},{1,2},{2,3},{3,4},{4,5},{5,6},{6,7},{7,0},{8,9},{9,10},{10,1... | collective-permute-start | bytes 786440 | tf_op jit(solution)/shard_map/ppermute | solution.py:37
  200.9 6.7 %collective-permute-start.17 = (bf16[256,512]{1,0:T(8,128)(2,1)S(1)}, bf16[256,512]{1,0:T(8,128)(2,1)S(1)}, u32[]{:S(2)}, u32[]{:S(2)}) collective-permute-start(bf16[256,512]{1,0:T(8,128)(2,1)S(1)} %collective-permute-done.16), channel_id=1, source_target_pairs={{0,1},{1,2},{2,3},{3,4},{4,5},{5,6},{6,7},{7,0},{8,9},{9,10},{10,1... | collective-permute-start | bytes 786440 | tf_op jit(solution)/shard_map/ppermute | solution.py:37
  214.3 6.8 %collective-permute-start.19 = (bf16[256,512]{1,0:T(8,128)(2,1)S(1)}, bf16[256,512]{1,0:T(8,128)(2,1)}, u32[]{:S(2)}, u32[]{:S(2)}) collective-permute-start(bf16[256,512]{1,0:T(8,128)(2,1)S(1)} %collective-permute-done.18), channel_id=1, source_target_pairs={{0,1},{1,2},{2,3},{3,4},{4,5},{5,6},{6,7},{7,0},{8,9},{9,10},{10,1... | collective-permute-start | bytes 786440 | tf_op jit(solution)/shard_map/ppermute | solution.py:37
  221.1 7.2 %collective-permute-start.20 = (bf16[256,512]{1,0:T(8,128)(2,1)}, bf16[256,512]{1,0:T(8,128)(2,1)}, u32[]{:S(2)}, u32[]{:S(2)}) collective-permute-start(bf16[256,512]{1,0:T(8,128)(2,1)} %collective-permute-done.19), channel_id=1, source_target_pairs={{0,1},{1,2},{2,3},{3,4},{4,5},{5,6},{6,7},{7,0},{8,9},{9,10},{10,1... | collective-permute-start | bytes 786440 | tf_op jit(solution)/shard_map/ppermute | solution.py:37
  262.6 6.7 %collective-permute-start.21 = (bf16[256,512]{1,0:T(8,128)(2,1)S(1)}, bf16[256,512]{1,0:T(8,128)(2,1)S(1)}, u32[]{:S(2)}, u32[]{:S(2)}) collective-permute-start(bf16[256,512]{1,0:T(8,128)(2,1)S(1)} %get-tuple-element.43), channel_id=1, source_target_pairs={{0,1},{1,2},{2,3},{3,4},{4,5},{5,6},{6,7},{7,0},{8,9},{9,10},{10,1... | collective-permute-start | bytes 786440 | tf_op jit(solution)/shard_map/ppermute | solution.py:37
  283.5 6.8 %collective-permute-start.24 = (bf16[256,512]{1,0:T(8,128)(2,1)S(1)}, bf16[256,512]{1,0:T(8,128)(2,1)}, u32[]{:S(2)}, u32[]{:S(2)}) collective-permute-start(bf16[256,512]{1,0:T(8,128)(2,1)S(1)} %collective-permute-done.23), channel_id=1, source_target_pairs={{0,1},{1,2},{2,3},{3,4},{4,5},{5,6},{6,7},{7,0},{8,9},{9,10},{10,1... | collective-permute-start | bytes 786440 | tf_op jit(solution)/shard_map/ppermute | solution.py:37
  290.3 7.0 %collective-permute-start.25 = (bf16[256,512]{1,0:T(8,128)(2,1)}, bf16[256,512]{1,0:T(8,128)(2,1)}, u32[]{:S(2)}, u32[]{:S(2)}) collective-permute-start(bf16[256,512]{1,0:T(8,128)(2,1)} %collective-permute-done.24), channel_id=1, source_target_pairs={{0,1},{1,2},{2,3},{3,4},{4,5},{5,6},{6,7},{7,0},{8,9},{9,10},{10,1... | collective-permute-start | bytes 786440 | tf_op jit(solution)/shard_map/ppermute | solution.py:37
  297.3 7.0 %collective-permute-start.26 = (bf16[256,512]{1,0:T(8,128)(2,1)}, bf16[256,512]{1,0:T(8,128)(2,1)}, u32[]{:S(2)}, u32[]{:S(2)}) collective-permute-start(bf16[256,512]{1,0:T(8,128)(2,1)} %collective-permute-done.25), channel_id=1, source_target_pairs={{0,1},{1,2},{2,3},{3,4},{4,5},{5,6},{6,7},{7,0},{8,9},{9,10},{10,1... | collective-permute-start | bytes 786440 | tf_op jit(solution)/shard_map/ppermute | solution.py:37
  304.3 7.1 %collective-permute-start.27 = (bf16[256,512]{1,0:T(8,128)(2,1)}, bf16[256,512]{1,0:T(8,128)(2,1)S(1)}, u32[]{:S(2)}, u32[]{:S(2)}) collective-permute-start(bf16[256,512]{1,0:T(8,128)(2,1)} %collective-permute-done.26), channel_id=1, source_target_pairs={{0,1},{1,2},{2,3},{3,4},{4,5},{5,6},{6,7},{7,0},{8,9},{9,10},{10,1... | collective-permute-start | bytes 786440 | tf_op jit(solution)/shard_map/ppermute | solution.py:37
  346.4 59.2 %all-to-all-start = ((bf16[4,256,512]{2,1,0:T(8,128)(2,1)}), bf16[4,256,512]{2,1,0:T(8,128)(2,1)S(1)}, u32[]{:S(2)}, u32[]{:S(2)}) async-start(bf16[4,256,512]{2,1,0:T(8,128)(2,1)} %select_convert_fusion), calls=%async_computation | async-start | bytes 2097152 | tf_op jit(solution)/shard_map/all_to_all | solution.py:113
  (46 other events, 611.7 us)
